TPU v7x, 128 devices: a whole 4x4x4 slice. The times are simulated.
128 devices in a mesh: gx: 8 (over z, core), gy: 16 (over y, x).
Axes of the slice: x: 4, y: 4, z: 4, core: 2. Of those that a mesh axis runs over, the one named last changes fastest.
Arguments:
- gradient: float32 [64, 4096], P('gx', 'gy'), may hold values from -6 to 6
- warm_start: float32 [64, 4096], P('gx', 'gy'), may hold values from -3 to 3
- viscosity: float32 [32, 64, 4096], P(None, 'gx', 'gy'), may hold values from 1 to 10
- friction_coef: float32 [64, 4096], P('gx', 'gy'), may hold values from 0.5 to 5
- slide_dir: float32 [2, 64, 4096], P(None, 'gx', 'gy'), may hold values from -4 to 4
- obs_weight: float32 [64, 4096], P('gx', 'gy'), may hold values from 0.5 to 2
- ice_mask: int32 [64, 4096], P('gx', 'gy'), may hold values 0 or 1
- grounded: int32 [64, 4096], P('gx', 'gy'), may hold values 0 or 1
Outputs:
- solution: float32 [64, 4096], P('gx', 'gy')
- residual: float32 [64, 4096], P('gx', 'gy')
All inputs are finite; a program needn't handle non-finite values. No bound on the sum of `ice_mask` or of `grounded` on one device may be relied on, other than what follows from the above.
Results may differ from a plain program's by a relative error of at most 0.00075.
Values sent between devices are 32-bit elements; how exact they have to be, the bound alone decides.
A program may use at most 128 MiB of HBM per device.

v0:
```python
import jax
import jax.numpy as jnp
from jax import lax
from jax.sharding import Mesh
from jax.sharding import PartitionSpec as P

ITERS = 2
GX_GY = ("gx_0", "gx_1", "gy_0", "gy_1")
GX = ("gx_0", "gx_1")
GY = ("gy_0", "gy_1")
vert_coupling = 128.0
sink_rate = 0.0625
bed_drag = 0.5
offset_weight = 0.0019
cross_share = 0.5
reg_gamma = 0.02
reg_smooth = 1.0
diag_scale = 0.003
neighbour_offsets = [
    (step_z, step_x, step_y)
    for step_z in (-1, 0, 1)
    for step_x in (-1, 0, 1)
    for step_y in (-1, 0, 1)
    if step_x != 0 or step_y != 0
]


def by_axis(value, axes):
    for axis in axes:
        value = lax.psum(value, axis)
    return value


def extended(block, sides, width):
    for axis, dim in sides:
        count = lax.axis_size(axis)
        forward = [(i, i + 1) for i in range(count - 1)]
        backward = [(target, source) for source, target in forward]
        low = lax.ppermute(
            lax.slice_in_dim(block, block.shape[dim] - width, None, axis=dim), axis, forward
        )
        high = lax.ppermute(lax.slice_in_dim(block, 0, width, axis=dim), axis, backward)
        block = jnp.concatenate([low, block, high], axis=dim)
    return block


def couple(field_ext, eta_ext):
    levels = eta_ext.shape[0]
    span_x = eta_ext.shape[1] - 2
    span_y = eta_ext.shape[2] - 2
    padded_field = jnp.pad(field_ext, ((0, 0), (1, 1), (0, 0), (0, 0)))
    padded_eta = jnp.pad(eta_ext, ((1, 1), (0, 0), (0, 0)))
    center = eta_ext[:, 1 : 1 + span_x, 1 : 1 + span_y]
    along_one = jnp.zeros((levels, span_x, span_y), jnp.float32)
    along_two = jnp.zeros((levels, span_x, span_y), jnp.float32)
    for step_z, step_x, step_y in neighbour_offsets:
        near_eta = padded_eta[
            1 + step_z : 1 + step_z + levels,
            1 + step_x : 1 + step_x + span_x,
            1 + step_y : 1 + step_y + span_y,
        ]
        weight = (
            offset_weight / (abs(step_x) + abs(step_y) + abs(step_z)) * 0.5 * (center + near_eta)
        )
        near_field = padded_field[
            :,
            1 + step_z : 1 + step_z + levels,
            1 + step_x : 1 + step_x + span_x,
            1 + step_y : 1 + step_y + span_y,
        ]
        along_one = along_one + weight * near_field[0]
        along_two = along_two + weight * near_field[1]
        if step_x != 0 and step_y != 0:
            twist_weight = cross_share * step_x * step_y * weight
            along_one = along_one + twist_weight * near_field[1]
            along_two = along_two + twist_weight * near_field[0]
    return jnp.stack([along_one, along_two])


def tridiagonal(link_weights, diagonal, rhs_cols):
    levels = diagonal.shape[0]
    pivot_value = diagonal[0]
    ratios = [-link_weights[0] / pivot_value]
    partial_value = [rhs_cols[:, 0] / pivot_value]
    for layer_index in range(1, levels):
        pivot_value = diagonal[layer_index] + link_weights[layer_index - 1] * ratios[-1]
        partial_value.append(
            (rhs_cols[:, layer_index] + link_weights[layer_index - 1] * partial_value[-1])
            / pivot_value
        )
        if layer_index < levels - 1:
            ratios.append(-link_weights[layer_index] / pivot_value)
    result = [partial_value[-1]]
    for layer_index in range(levels - 2, -1, -1):
        result.insert(0, partial_value[layer_index] - ratios[layer_index] * result[0])
    return jnp.stack(result, axis=1)


def responses(viscosity, friction):
    levels = viscosity.shape[0]
    link_weights = vert_coupling * 0.5 * (viscosity[:-1] + viscosity[1:])
    zero_layer = jnp.zeros_like(viscosity[:1])
    diagonal = (
        jnp.concatenate([zero_layer, link_weights])
        + jnp.concatenate([link_weights, zero_layer])
        + sink_rate * viscosity
    )
    diagonal = diagonal.at[0].add(bed_drag * friction)
    unit_rhs = jnp.zeros((2,) + viscosity.shape, jnp.float32)
    unit_rhs = unit_rhs.at[0, 0].set(1.0).at[1, levels - 1].set(1.0)
    solved = tridiagonal(link_weights, diagonal, unit_rhs)
    return (solved[0], solved[1])


def regularize(centre_ext):
    middle = centre_ext[1:-1, 1:-1]
    beside_all = (
        centre_ext[2:, 1:-1] + centre_ext[:-2, 1:-1] + centre_ext[1:-1, 2:] + centre_ext[1:-1, :-2]
    )
    return reg_gamma * (middle + reg_smooth * (4.0 * middle - beside_all))


def paired_dots(residual, precond, image_vec):
    return (
        by_axis(jnp.sum(residual * precond), GX_GY),
        by_axis(jnp.sum(precond * image_vec), GX_GY),
    )


def on_device(
    gradient, warm_start, viscosity, friction_coef, slide_dir, obs_weight, ice_mask, grounded
):
    ice_float = ice_mask.astype(jnp.float32)
    ground_float = grounded.astype(jnp.float32)
    friction = ground_float * friction_coef
    source = (ice_float * ground_float * friction_coef)[None] * slide_dir
    obs = ice_float * obs_weight
    inverse_diag = 1.0 / (
        reg_gamma * (1.0 + 4.0 * reg_smooth)
        + diag_scale * ice_float * ground_float * friction_coef * friction_coef
    )
    viscosity_wide = extended(viscosity, ((GX, 1), (GY, 2)), 2)
    columns = jnp.concatenate([source, obs[None], friction[None]], axis=0)
    column_wide = extended(columns, ((GX, 1), (GY, 2)), 2)
    safe_eta = jnp.where(viscosity_wide > 0.0, viscosity_wide, 1.0)
    bottom_wide, top_wide = responses(safe_eta, column_wide[3])
    bottom_inner = bottom_wide[:, 1:-1, 1:-1]
    top_inner = top_wide[:, 1:-1, 1:-1]
    bottom_own = bottom_wide[:, 2:-2, 2:-2]
    top_own = top_wide[:, 2:-2, 2:-2]

    def hessian(direction):
        wide_dir = extended(direction, ((GX, 0), (GY, 1)), 2)
        spread = column_wide[:2] * wide_dir[None]
        first_state = bottom_wide[None] * spread[:, None]
        coupled = couple(first_state, viscosity_wide)
        surface = spread[:, 1:-1, 1:-1] * bottom_inner[-1][None] + jnp.sum(
            top_inner[None] * coupled, axis=1
        )
        traction = column_wide[2, 1:-1, 1:-1][None] * surface
        second_state = top_inner[None] * traction[:, None]
        coupled_back = couple(second_state, viscosity_wide[:, 1:-1, 1:-1])
        basal_part = traction[:, 1:-1, 1:-1] * top_own[0][None] + jnp.sum(
            bottom_own[None] * coupled_back, axis=1
        )
        return jnp.sum(source * basal_part, axis=0) + regularize(wide_dir[1:-1, 1:-1])

    solution = warm_start
    residual = gradient - hessian(warm_start)
    precond = inverse_diag * residual
    image_vec = hessian(precond)
    norm_now, product = paired_dots(residual, precond, image_vec)
    step_size = norm_now / product
    direction = precond
    along_dir = image_vec
    for iteration in range(ITERS):
        solution = solution + step_size * direction
        residual = residual - step_size * along_dir
        if iteration + 1 < ITERS:
            precond = inverse_diag * residual
            image_vec = hessian(precond)
            norm_next, product = paired_dots(residual, precond, image_vec)
            ratio_cg = norm_next / norm_now
            step_size = norm_next / (product - ratio_cg * norm_next / step_size)
            direction = precond + ratio_cg * direction
            along_dir = image_vec + ratio_cg * along_dir
            norm_now = norm_next
    return (solution, residual)


def solution(mesh):
    finer = Mesh(mesh.devices.reshape(4, 2, 4, 4), ("gx_0", "gx_1", "gy_0", "gy_1"))
    return jax.shard_map(
        on_device,
        mesh=finer,
        in_specs=(
            P(GX, GY),
            P(GX, GY),
            P(None, GX, GY),
            P(GX, GY),
            P(None, GX, GY),
            P(GX, GY),
            P(GX, GY),
            P(GX, GY),
        ),
        out_specs=(P(GX, GY), P(GX, GY)),
        check_vma=False,
    )
```

profile of v0, /device:TPU:8, one launch (start us, length us, event | category | flops | bytes accessed | tf_op | source)
XLA Modules:
  0.0 279.2 jit_solution(12042140770638936635)
XLA Ops:
  5.9 4.9 %collective-permute-start = (f32[4,2,256]{2,1,0:T(2,128)S(1)}, f32[4,2,256]{2,1,0:T(2,128)S(1)}, u32[]{:S(2)}, u32[]{:S(2)}) collective-permute-start(f32[4,2,256]{2,1,0:T(2,128)S(1)} %get-tuple-element.246), channel_id=1, source_target_pairs={{0,16},{16,32},{32,48},{48,64},{64,80},{80,96},{96,112},{1,17},{17... | collective-permute-start | bytes 24584 | tf_op jit(solution)/shard_map/ppermute | solution.py:39
  13.2 4.3 %collective-permute-start.8 = (f32[32,2,256]{2,1,0:T(2,128)S(1)}, f32[32,2,256]{2,1,0:T(2,128)S(1)}, u32[]{:S(2)}, u32[]{:S(2)}) collective-permute-start(f32[32,2,256]{2,1,0:T(2,128)S(1)} %get-tuple-element.242), channel_id=1, source_target_pairs={{0,16},{16,32},{32,48},{48,64},{64,80},{80,96},{96,112},{1,17},{17... | collective-permute-start | bytes 196616 | tf_op jit(solution)/shard_map/ppermute | solution.py:39
  23.0 4.6 %collective-permute-start.7 = (f32[12,2]{1,0:T(8,128)S(1)}, f32[12,2]{1,0:T(8,128)S(1)}, u32[]{:S(2)}, u32[]{:S(2)}) collective-permute-start(f32[12,2]{1,0:T(8,128)S(1)} %get-tuple-element.253), channel_id=1, source_target_pairs={{1,0},{2,1},{3,2},{4,3},{5,4},{6,5},{7,6},{8,7},{9,8},{10,9},{11,1... | collective-permute-start | bytes 296 | tf_op jit(solution)/shard_map/ppermute | solution.py:42
  29.6 6.0 %collective-permute-start.3 = (f32[4,12,2]{2,1,0:T(8,128)S(1)}, f32[4,12,2]{2,1,0:T(8,128)S(1)}, u32[]{:S(2)}, u32[]{:S(2)}) collective-permute-start(f32[4,12,2]{2,1,0:T(8,128)S(1)} %get-tuple-element.245), channel_id=1, source_target_pairs={{1,0},{2,1},{3,2},{4,3},{5,4},{6,5},{7,6},{8,7},{9,8},{10,9},{11,1... | collective-permute-start | bytes 1160 | tf_op jit(solution)/shard_map/ppermute | solution.py:42
  41.1 6.3 %collective-permute-start.11 = (f32[32,12,2]{2,1,0:T(8,128)S(1)}, f32[32,12,2]{2,1,0:T(8,128)S(1)}, u32[]{:S(2)}, u32[]{:S(2)}) collective-permute-start(f32[32,12,2]{2,1,0:T(8,128)S(1)} %get-tuple-element.239), channel_id=1, source_target_pairs={{1,0},{2,1},{3,2},{4,3},{5,4},{6,5},{7,6},{8,7},{9,8},{10,9},{11,1... | collective-permute-start | bytes 9224 | tf_op jit(solution)/shard_map/ppermute | solution.py:42
  48.2 4.2 %collective-permute-done.10 = f32[32,12,2]{2,1,0:T(8,128)S(1)} collective-permute-done((f32[32,12,2]{2,1,0:T(8,128)S(1)}, f32[32,12,2]{2,1,0:T(8,128)S(1)}, u32[]{:S(2)}, u32[]{:S(2)}) %collective-permute-start.10) | collective-permute-done | bytes 3104 | tf_op jit(solution)/shard_map/ppermute | solution.py:39
  60.6 9.6 %fusion.241 = (f32[1,32,10,258]{3,2,1,0:T(8,128)}, f32[32,10,258]{2,1,0:T(8,128)S(1)}, f32[32,10,258]{2,1,0:T(8,128)S(1)}, f32[32,10,258]{2,1,0:T(8,128)S(1)}, f...) fusion(f32[2,32,12,260]{3,2,1,0:T(8,128)S(1)} %broadcast_multip, ...), kind=kLoop, calls=%fused_computation.521 | loop fusion | flops 10815360 | bytes 27130368 | tf_op jit(solution)/shard_map/stack | solution.py:77
  70.2 9.7 %fusion.242 = f32[1,32,10,258]{3,2,1,0:T(8,128)} fusion(f32[32,10,258]{2,1,0:T(8,128)} %get-tuple-element.109, f32[32,10,258]{2,1,0:T(8,128)} %get-tuple-element.108, f32[32,10,258]{2,1,0:T(8,128)} %get-tuple-element.107, f32[32,10,258]{2,1,0:T(8,128)} %get-tuple-element.106, f32[32,10,258]{2,1,0:T(8,128)} %get-tuple-element.105, ...), kind=kLoop, calls=%fused_computation.522 | loop fusion | flops 7843200 | bytes 22459392 | tf_op jit(solution)/shard_map/stack | solution.py:77
  83.3 4.4 %fusion.518 = (f32[1,32,8,256]{3,2,1,0:T(8,128)}, f32[32,8,256]{2,1,0:T(8,128)}, f32[32,8,256]{2,1,0:T(8,128)}, f32[32,8,256]{2,1,0:T(8,128)}, f32[32,8,256]{2,1...) fusion(f32[2,32,10,258]{3,2,1,0:T(8,128)S(1)} %broadcast_multip, ...), kind=kLoop, calls=%fused_computation.1103 | loop fusion | flops 8716288 | bytes 13500416 | tf_op jit(solution)/shard_map/stack | solution.py:77
  87.7 4.5 %fusion.515 = f32[1,32,8,256]{3,2,1,0:T(8,128)} fusion(f32[32,8,256]{2,1,0:T(8,128)} %get-tuple-element.84, f32[32,8,256]{2,1,0:T(8,128)} %get-tuple-element.83, f32[32,8,256]{2,1,0:T(8,128)} %get-tuple-element.82, f32[32,8,256]{2,1,0:T(8,128)} %get-tuple-element.81, f32[2,32,10,258]{3,2,1,0:T(8,128)S(1)} %broadcast_multiply_fusion.4, ...), kind=kLoop, calls=%fused_computation.1100 | loop fusion | flops 6619136 | bytes 11141120 | tf_op jit(solution)/shard_map/stack | solution.py:77
  106.6 4.7 %collective-permute-start.15 = (f32[12,2]{1,0:T(8,128)S(1)}, f32[12,2]{1,0:T(8,128)S(1)}, u32[]{:S(2)}, u32[]{:S(2)}) collective-permute-start(f32[12,2]{1,0:T(8,128)S(1)} %get-tuple-element.251), channel_id=1, source_target_pairs={{1,0},{2,1},{3,2},{4,3},{5,4},{6,5},{7,6},{8,7},{9,8},{10,9},{11,1... | collective-permute-start | bytes 296 | tf_op jit(solution)/shard_map/ppermute | solution.py:42
  116.0 8.7 %fusion.244 = f32[1,32,10,258]{3,2,1,0:T(8,128)} fusion(f32[32,10,258]{2,1,0:T(8,128)} %get-tuple-element.109, f32[32,10,258]{2,1,0:T(8,128)} %get-tuple-element.108, f32[32,10,258]{2,1,0:T(8,128)} %get-tuple-element.107, f32[32,10,258]{2,1,0:T(8,128)} %get-tuple-element.106, f32[32,10,258]{2,1,0:T(8,128)} %get-tuple-element.105, ...), kind=kLoop, calls=%fused_computation.524 | loop fusion | flops 7843200 | bytes 22459392 | tf_op jit(solution)/shard_map/stack | solution.py:77
  124.7 8.6 %fusion.243 = f32[1,32,10,258]{3,2,1,0:T(8,128)} fusion(f32[32,10,258]{2,1,0:T(8,128)} %get-tuple-element.109, f32[32,10,258]{2,1,0:T(8,128)} %get-tuple-element.108, f32[32,10,258]{2,1,0:T(8,128)} %get-tuple-element.107, f32[32,10,258]{2,1,0:T(8,128)} %get-tuple-element.106, f32[32,10,258]{2,1,0:T(8,128)} %get-tuple-element.105, ...), kind=kLoop, calls=%fused_computation.523 | loop fusion | flops 7843200 | bytes 22459392 | tf_op jit(solution)/shard_map/stack | solution.py:77
  135.8 4.5 %fusion.516 = f32[1,32,8,256]{3,2,1,0:T(8,128)} fusion(f32[32,8,256]{2,1,0:T(8,128)} %get-tuple-element.84, f32[32,8,256]{2,1,0:T(8,128)} %get-tuple-element.83, f32[32,8,256]{2,1,0:T(8,128)} %get-tuple-element.82, f32[32,8,256]{2,1,0:T(8,128)} %get-tuple-element.81, f32[2,32,10,258]{3,2,1,0:T(8,128)S(1)} %broadcast_multiply_fusion.2, ...), kind=kLoop, calls=%fused_computation.1101 | loop fusion | flops 6619136 | bytes 11141120 | tf_op jit(solution)/shard_map/stack | solution.py:77
  140.3 4.5 %fusion.519 = f32[1,32,8,256]{3,2,1,0:T(8,128)} fusion(f32[32,8,256]{2,1,0:T(8,128)} %get-tuple-element.84, f32[2,32,10,258]{3,2,1,0:T(8,128)S(1)} %broadcast_multiply_fusion.2, f32[32,8,256]{2,1,0:T(8,128)} %get-tuple-element.83, f32[32,8,256]{2,1,0:T(8,128)} %get-tuple-element.82, f32[32,8,256]{2,1,0:T(8,128)} %get-tuple-element.81, ...), kind=kLoop, calls=%fused_computation.1104 | loop fusion | flops 6619136 | bytes 11141120 | tf_op jit(solution)/shard_map/stack | solution.py:77
  149.0 12.6 %all-reduce.15 = (f32[]{:T(128)}, f32[]{:T(128)}) all-reduce(f32[]{:T(128)} %get-tuple-element.41, f32[]{:T(128)} %get-tuple-element.40), channel_id=1, replica_groups=mesh['gx_0'=4,'gx_1'=2,'gy_0'=4,'gy_1'=4] {'gx_0'}, use_global_device_ids=true, to_apply=%region_4.5 | all-reduce | flops 2 | bytes 16 | tf_op jit(solution)/shard_map/psum | solution.py:30
  164.7 9.4 %all-reduce.13 = (f32[]{:T(128)}, f32[]{:T(128)}) all-reduce(f32[]{:T(128)} %get-tuple-element.56, f32[]{:T(128)} %get-tuple-element.57), channel_id=1, replica_groups=mesh['gx_0'=4,'gx_1'=2,'gy_0'=4,'gy_1'=4] {'gy_0'}, use_global_device_ids=true, to_apply=%region_6.7 | all-reduce | flops 2 | bytes 16 | tf_op jit(solution)/shard_map/psum | solution.py:30
  174.1 12.6 %all-reduce.11 = (f32[]{:T(128)}, f32[]{:T(128)}) all-reduce(f32[]{:T(128)} %get-tuple-element.48, f32[]{:T(128)} %get-tuple-element.49), channel_id=1, replica_groups=mesh['gx_0'=4,'gx_1'=2,'gy_0'=4,'gy_1'=4] {'gy_1'}, use_global_device_ids=true, to_apply=%region_7.8 | all-reduce | flops 2 | bytes 16 | tf_op jit(solution)/shard_map/psum | solution.py:30
  195.3 6.3 %collective-permute-start.19 = (f32[12,2]{1,0:T(8,128)S(1)}, f32[12,2]{1,0:T(8,128)S(1)}, u32[]{:S(2)}, u32[]{:S(2)}) collective-permute-start(f32[12,2]{1,0:T(8,128)S(1)} %get-tuple-element.249), channel_id=1, source_target_pairs={{1,0},{2,1},{3,2},{4,3},{5,4},{6,5},{7,6},{8,7},{9,8},{10,9},{11,1... | collective-permute-start | bytes 296 | tf_op jit(solution)/shard_map/ppermute | solution.py:42
  205.5 8.8 %fusion.246 = f32[1,32,10,258]{3,2,1,0:T(8,128)} fusion(f32[32,10,258]{2,1,0:T(8,128)} %get-tuple-element.109, f32[32,10,258]{2,1,0:T(8,128)} %get-tuple-element.108, f32[32,10,258]{2,1,0:T(8,128)} %get-tuple-element.107, f32[32,10,258]{2,1,0:T(8,128)} %get-tuple-element.106, f32[32,10,258]{2,1,0:T(8,128)} %get-tuple-element.105, ...), kind=kLoop, calls=%fused_computation.526 | loop fusion | flops 7843200 | bytes 22003200 | tf_op jit(solution)/shard_map/stack | solution.py:77
  214.3 8.6 %fusion.245 = f32[1,32,10,258]{3,2,1,0:T(8,128)} fusion(f32[32,10,258]{2,1,0:T(8,128)} %get-tuple-element.109, f32[32,10,258]{2,1,0:T(8,128)} %get-tuple-element.108, f32[32,10,258]{2,1,0:T(8,128)} %get-tuple-element.107, f32[32,10,258]{2,1,0:T(8,128)} %get-tuple-element.106, f32[32,10,258]{2,1,0:T(8,128)} %get-tuple-element.105, ...), kind=kLoop, calls=%fused_computation.525 | loop fusion | flops 7843200 | bytes 22459392 | tf_op jit(solution)/shard_map/stack | solution.py:77
  238.0 10.6 %all-reduce.14 = (f32[]{:T(128)}, f32[]{:T(128)}) all-reduce(f32[]{:T(128)} %get-tuple-element.39, f32[]{:T(128)} %get-tuple-element.38), channel_id=1, replica_groups=mesh['gx_0'=4,'gx_1'=2,'gy_0'=4,'gy_1'=4] {'gx_0'}, use_global_device_ids=true, to_apply=%region_17.18 | all-reduce | flops 2 | bytes 16 | tf_op jit(solution)/shard_map/psum | solution.py:30
  251.7 7.9 %all-reduce.12 = (f32[]{:T(128)}, f32[]{:T(128)}) all-reduce(f32[]{:T(128)} %get-tuple-element.54, f32[]{:T(128)} %get-tuple-element.55), channel_id=1, replica_groups=mesh['gx_0'=4,'gx_1'=2,'gy_0'=4,'gy_1'=4] {'gy_0'}, use_global_device_ids=true, to_apply=%region_19.20 | all-reduce | flops 2 | bytes 16 | tf_op jit(solution)/shard_map/psum | solution.py:30
  259.5 13.8 %all-reduce.10 = (f32[]{:T(128)}, f32[]{:T(128)}) all-reduce(f32[]{:T(128)} %get-tuple-element.46, f32[]{:T(128)} %get-tuple-element.47), channel_id=1, replica_groups=mesh['gx_0'=4,'gx_1'=2,'gy_0'=4,'gy_1'=4] {'gy_1'}, use_global_device_ids=true, to_apply=%region_20.21 | all-reduce | flops 2 | bytes 16 | tf_op jit(solution)/shard_map/psum | solution.py:30
  (276 shorter events, 91.2 us)
Async XLA Ops:
  1.4 16.1 %collective-permute-start.4 = (f32[2,256]{1,0:T(2,128)S(1)}, f32[2,256]{1,0:T(2,128)S(1)}, u32[]{:S(2)}, u32[]{:S(2)}) collective-permute-start(f32[2,256]{1,0:T(2,128)S(1)} %get-tuple-element.261), channel_id=1, source_target_pairs={{0,16},{16,32},{32,48},{48,64},{64,80},{80,96},{96,112},{1,17},{17... | collective-permute-start | bytes 6152 | tf_op jit(solution)/shard_map/ppermute | solution.py:39
  3.1 15.7 %collective-permute-start.5 = (f32[2,256]{1,0:T(2,128)S(1)}, f32[2,256]{1,0:T(2,128)S(1)}, u32[]{:S(2)}, u32[]{:S(2)}) collective-permute-start(f32[2,256]{1,0:T(2,128)S(1)} %get-tuple-element.262), channel_id=1, source_target_pairs={{16,0},{32,16},{48,32},{64,48},{80,64},{96,80},{112,96},{17,1},{33... | collective-permute-start | bytes 6152 | tf_op jit(solution)/shard_map/ppermute | solution.py:42
  5.2 88.3 %copy-start.51 = (f32[8,256]{1,0:T(8,128)}, f32[8,256]{1,0:T(8,128)S(1)}, u32[]{:S(2)}) copy-start(f32[8,256]{1,0:T(8,128)S(1)} %get-tuple-element.255) | copy-start | bytes 24580
  5.9 47.6 %copy-start.12 = (f32[32,8,256]{2,1,0:T(8,128)S(1)}, f32[32,8,256]{2,1,0:T(8,128)}, u32[]{:S(2)}) copy-start(f32[32,8,256]{2,1,0:T(8,128)} %param.16) | copy-start | bytes 786436
  5.9 17.1 %collective-permute-start = (f32[4,2,256]{2,1,0:T(2,128)S(1)}, f32[4,2,256]{2,1,0:T(2,128)S(1)}, u32[]{:S(2)}, u32[]{:S(2)}) collective-permute-start(f32[4,2,256]{2,1,0:T(2,128)S(1)} %get-tuple-element.246), channel_id=1, source_target_pairs={{0,16},{16,32},{32,48},{48,64},{64,80},{80,96},{96,112},{1,17},{17... | collective-permute-start | bytes 24584 | tf_op jit(solution)/shard_map/ppermute | solution.py:39
  10.8 16.8 %collective-permute-start.1 = (f32[4,2,256]{2,1,0:T(2,128)S(1)}, f32[4,2,256]{2,1,0:T(2,128)S(1)}, u32[]{:S(2)}, u32[]{:S(2)}) collective-permute-start(f32[4,2,256]{2,1,0:T(2,128)S(1)} %get-tuple-element.247), channel_id=1, source_target_pairs={{16,0},{32,16},{48,32},{64,48},{80,64},{96,80},{112,96},{17,1},{33... | collective-permute-start | bytes 24584 | tf_op jit(solution)/shard_map/ppermute | solution.py:42
  13.2 24.2 %collective-permute-start.8 = (f32[32,2,256]{2,1,0:T(2,128)S(1)}, f32[32,2,256]{2,1,0:T(2,128)S(1)}, u32[]{:S(2)}, u32[]{:S(2)}) collective-permute-start(f32[32,2,256]{2,1,0:T(2,128)S(1)} %get-tuple-element.242), channel_id=1, source_target_pairs={{0,16},{16,32},{32,48},{48,64},{64,80},{80,96},{96,112},{1,17},{17... | collective-permute-start | bytes 196616 | tf_op jit(solution)/shard_map/ppermute | solution.py:39
  17.5 36.6 %copy-start.60 = (f32[2,256]{1,0:T(2,128)}, f32[2,256]{1,0:T(2,128)S(1)}, u32[]{:S(2)}) copy-start(f32[2,256]{1,0:T(2,128)S(1)} %collective-permute-done.4) | copy-start | bytes 6148
  17.5 20.5 %collective-permute-start.9 = (f32[32,2,256]{2,1,0:T(2,128)S(1)}, f32[32,2,256]{2,1,0:T(2,128)S(1)}, u32[]{:S(2)}, u32[]{:S(2)}) collective-permute-start(f32[32,2,256]{2,1,0:T(2,128)S(1)} %get-tuple-element.243), channel_id=1, source_target_pairs={{16,0},{32,16},{48,32},{64,48},{80,64},{96,80},{112,96},{17,1},{33... | collective-permute-start | bytes 196616 | tf_op jit(solution)/shard_map/ppermute | solution.py:42
  19.6 10.0 %collective-permute-start.6 = (f32[12,2]{1,0:T(8,128)S(1)}, f32[12,2]{1,0:T(8,128)S(1)}, u32[]{:S(2)}, u32[]{:S(2)}) collective-permute-start(f32[12,2]{1,0:T(8,128)S(1)} %get-tuple-element.252), channel_id=1, source_target_pairs={{0,1},{1,2},{2,3},{3,4},{4,5},{5,6},{6,7},{7,8},{8,9},{9,10},{10,1... | collective-permute-start | bytes 296 | tf_op jit(solution)/shard_map/ppermute | solution.py:39
  23.0 12.7 %collective-permute-start.7 = (f32[12,2]{1,0:T(8,128)S(1)}, f32[12,2]{1,0:T(8,128)S(1)}, u32[]{:S(2)}, u32[]{:S(2)}) collective-permute-start(f32[12,2]{1,0:T(8,128)S(1)} %get-tuple-element.253), channel_id=1, source_target_pairs={{1,0},{2,1},{3,2},{4,3},{5,4},{6,5},{7,6},{8,7},{9,8},{10,9},{11,1... | collective-permute-start | bytes 296 | tf_op jit(solution)/shard_map/ppermute | solution.py:42
  27.7 8.8 %collective-permute-start.2 = (f32[4,12,2]{2,1,0:T(8,128)S(1)}, f32[4,12,2]{2,1,0:T(8,128)S(1)}, u32[]{:S(2)}, u32[]{:S(2)}) collective-permute-start(f32[4,12,2]{2,1,0:T(8,128)S(1)} %get-tuple-element.244), channel_id=1, source_target_pairs={{0,1},{1,2},{2,3},{3,4},{4,5},{5,6},{6,7},{7,8},{8,9},{9,10},{10,1... | collective-permute-start | bytes 1160 | tf_op jit(solution)/shard_map/ppermute | solution.py:39
  29.6 7.6 %collective-permute-start.3 = (f32[4,12,2]{2,1,0:T(8,128)S(1)}, f32[4,12,2]{2,1,0:T(8,128)S(1)}, u32[]{:S(2)}, u32[]{:S(2)}) collective-permute-start(f32[4,12,2]{2,1,0:T(8,128)S(1)} %get-tuple-element.245), channel_id=1, source_target_pairs={{1,0},{2,1},{3,2},{4,3},{5,4},{6,5},{7,6},{8,7},{9,8},{10,9},{11,1... | collective-permute-start | bytes 1160 | tf_op jit(solution)/shard_map/ppermute | solution.py:42
  39.2 13.2 %collective-permute-start.10 = (f32[32,12,2]{2,1,0:T(8,128)S(1)}, f32[32,12,2]{2,1,0:T(8,128)S(1)}, u32[]{:S(2)}, u32[]{:S(2)}) collective-permute-start(f32[32,12,2]{2,1,0:T(8,128)S(1)} %get-tuple-element.238), channel_id=1, source_target_pairs={{0,1},{1,2},{2,3},{3,4},{4,5},{5,6},{6,7},{7,8},{8,9},{9,10},{10,1... | collective-permute-start | bytes 9224 | tf_op jit(solution)/shard_map/ppermute | solution.py:39
  41.1 12.4 %collective-permute-start.11 = (f32[32,12,2]{2,1,0:T(8,128)S(1)}, f32[32,12,2]{2,1,0:T(8,128)S(1)}, u32[]{:S(2)}, u32[]{:S(2)}) collective-permute-start(f32[32,12,2]{2,1,0:T(8,128)S(1)} %get-tuple-element.239), channel_id=1, source_target_pairs={{1,0},{2,1},{3,2},{4,3},{5,4},{6,5},{7,6},{8,7},{9,8},{10,9},{11,1... | collective-permute-start | bytes 9224 | tf_op jit(solution)/shard_map/ppermute | solution.py:42
  96.1 50.7 %copy-start.50 = (f32[8,256]{1,0:T(8,128)}, f32[8,256]{1,0:T(8,128)S(1)}, u32[]{:S(2)}) copy-start(f32[8,256]{1,0:T(8,128)S(1)} %get-tuple-element.60) | copy-start | bytes 24580
  96.2 2.7 collective-permute-start.12
  97.6 5.1 %collective-permute-start.13 = (f32[2,256]{1,0:T(2,128)S(1)}, f32[2,256]{1,0:T(2,128)S(1)}, u32[]{:S(2)}, u32[]{:S(2)}) collective-permute-start(f32[2,256]{1,0:T(2,128)S(1)} %get-tuple-element.260), channel_id=1, source_target_pairs={{16,0},{32,16},{48,32},{64,48},{80,64},{96,80},{112,96},{17,1},{33... | collective-permute-start | bytes 6152 | tf_op jit(solution)/shard_map/ppermute | solution.py:42
  102.7 8.6 %collective-permute-start.14 = (f32[12,2]{1,0:T(8,128)S(1)}, f32[12,2]{1,0:T(8,128)S(1)}, u32[]{:S(2)}, u32[]{:S(2)}) collective-permute-start(f32[12,2]{1,0:T(8,128)S(1)} %get-tuple-element.250), channel_id=1, source_target_pairs={{0,1},{1,2},{2,3},{3,4},{4,5},{5,6},{6,7},{7,8},{8,9},{9,10},{10,1... | collective-permute-start | bytes 296 | tf_op jit(solution)/shard_map/ppermute | solution.py:39
  106.6 6.1 %collective-permute-start.15 = (f32[12,2]{1,0:T(8,128)S(1)}, f32[12,2]{1,0:T(8,128)S(1)}, u32[]{:S(2)}, u32[]{:S(2)}) collective-permute-start(f32[12,2]{1,0:T(8,128)S(1)} %get-tuple-element.251), channel_id=1, source_target_pairs={{1,0},{2,1},{3,2},{4,3},{5,4},{6,5},{7,6},{8,7},{9,8},{10,9},{11,1... | collective-permute-start | bytes 296 | tf_op jit(solution)/shard_map/ppermute | solution.py:42
  188.9 2.6 collective-permute-start.16
  190.2 3.1 %collective-permute-start.17 = (f32[2,256]{1,0:T(2,128)S(1)}, f32[2,256]{1,0:T(2,128)S(1)}, u32[]{:S(2)}, u32[]{:S(2)}) collective-permute-start(f32[2,256]{1,0:T(2,128)S(1)} %get-tuple-element.258), channel_id=1, source_target_pairs={{16,0},{32,16},{48,32},{64,48},{80,64},{96,80},{112,96},{17,1},{33... | collective-permute-start | bytes 6152 | tf_op jit(solution)/shard_map/ppermute | solution.py:42
  193.4 8.2 %collective-permute-start.18 = (f32[12,2]{1,0:T(8,128)S(1)}, f32[12,2]{1,0:T(8,128)S(1)}, u32[]{:S(2)}, u32[]{:S(2)}) collective-permute-start(f32[12,2]{1,0:T(8,128)S(1)} %get-tuple-element.248), channel_id=1, source_target_pairs={{0,1},{1,2},{2,3},{3,4},{4,5},{5,6},{6,7},{7,8},{8,9},{9,10},{10,1... | collective-permute-start | bytes 296 | tf_op jit(solution)/shard_map/ppermute | solution.py:39
  195.3 7.4 %collective-permute-start.19 = (f32[12,2]{1,0:T(8,128)S(1)}, f32[12,2]{1,0:T(8,128)S(1)}, u32[]{:S(2)}, u32[]{:S(2)}) collective-permute-start(f32[12,2]{1,0:T(8,128)S(1)} %get-tuple-element.249), channel_id=1, source_target_pairs={{1,0},{2,1},{3,2},{4,3},{5,4},{6,5},{7,6},{8,7},{9,8},{10,9},{11,1... | collective-permute-start | bytes 296 | tf_op jit(solution)/shard_map/ppermute | solution.py:42
  (62 other events, 457.8 us)
where the time goes:
time: 281 us; the launch traced here: 279 us
  other arithmetic  111 us (40%)
  blocking collectives  73 us (26%)
  starting transfers between devices  60.9 us (22%)
  waiting for transfers between devices  14.1 us (5%)
  local copies, waits for them, and re-layouts  12.1 us (4%)
  between operations  7.96 us (3%)
    another operation x12, other arithmetic, couple(): return jnp.stack([along_one, along_two])  80.1 us
    psum x8, blocking collectives, by_axis(): value = lax.psum(value, axis)  73 us
    ppermute x10, starting transfers between devices, extended(): lax.ppermute(lax.slice_in_dim(block, 0, width, axis=dim), axis, backward)  34.3 us
    ppermute x10, starting transfers between devices, extended(): lax.ppermute(lax.slice_in_dim(block, block.shape[dim] - width, None, axis...  26.6 us
    ppermute x10, waiting for transfers between devices, extended(): lax.ppermute(lax.slice_in_dim(block, 0, width, axis=dim), axis, backward)  9.88 us
    unnamed x147, local copies, waits for them, and re-layouts  6.45 us
  transfers between devices with their start and end apart: 20, of which 7 were waited for; matrix products, arithmetic and copies ran while one was open for 2% of the time, Pallas kernels for 0%

commit v1 on v0

--- a/solution.py
+++ b/solution.py
@@ -27,7 +27,7 @@
 
 def by_axis(value, axes):
     for axis in axes:
-        value = lax.psum(value, axis)
+        value = jnp.sum(lax.all_gather(value, axis), axis=0)
     return value
 
 

time: 281 us -> 335 us (1.19)
  local copies, waits for them, and re-layouts: 12.1 us -> 52.8 us
  other arithmetic: 111 us -> 127 us
    psum x8 -> x0, blocking collectives: 73 us -> none  [by_axis(): value = lax.psum(value, axis)]
    unnamed x0 -> x8, blocking collectives: none -> 70.4 us
    unnamed x147 -> x183, local copies, waits for them, and re-layouts: 6.45 us -> 46.6 us
    reduce_sum x0 -> x16, other arithmetic: none -> 14.7 us  [by_axis(): value = jnp.sum(lax.all_gather(value, axis), axis=0)]
where the time goes in v1:
time: 335 us; the launch traced here: 332 us
  other arithmetic  127 us (38%)
  blocking collectives  70.4 us (21%)
  starting transfers between devices  61.5 us (18%)
  local copies, waits for them, and re-layouts  52.8 us (16%)
  waiting for transfers between devices  12.4 us (4%)
  between operations  8.17 us (2%)
    another operation x12, other arithmetic, couple(): return jnp.stack([along_one, along_two])  80.2 us
    unnamed x8, blocking collectives  70.4 us
    unnamed x183, local copies, waits for them, and re-layouts  46.6 us
    ppermute x10, starting transfers between devices, extended(): lax.ppermute(lax.slice_in_dim(block, 0, width, axis=dim), axis, backward)  34.3 us
    ppermute x10, starting transfers between devices, extended(): lax.ppermute(lax.slice_in_dim(block, block.shape[dim] - width, None, axis...  27.2 us
    reduce_sum x16, other arithmetic, by_axis(): value = jnp.sum(lax.all_gather(value, axis), axis=0)  14.7 us
    ppermute x10, waiting for transfers between devices, extended(): lax.ppermute(lax.slice_in_dim(block, 0, width, axis=dim), axis, backward)  8.15 us
  transfers between devices with their start and end apart: 20, of which 7 were waited for; matrix products, arithmetic and copies ran while one was open for 2% of the time, Pallas kernels for 0%

profile of v1, /device:TPU:8, one launch (start us, length us, event | category | flops | bytes accessed | tf_op | source)
XLA Modules:
  0.0 332.4 jit_solution(7826285369001129612)
XLA Ops:
  5.9 4.9 %collective-permute-start = (f32[4,2,256]{2,1,0:T(2,128)S(1)}, f32[4,2,256]{2,1,0:T(2,128)S(1)}, u32[]{:S(2)}, u32[]{:S(2)}) collective-permute-start(f32[4,2,256]{2,1,0:T(2,128)S(1)} %get-tuple-element.246), channel_id=1, source_target_pairs={{0,16},{16,32},{32,48},{48,64},{64,80},{80,96},{96,112},{1,17},{17... | collective-permute-start | bytes 24584 | tf_op jit(solution)/shard_map/ppermute | solution.py:39
  13.2 4.3 %collective-permute-start.8 = (f32[32,2,256]{2,1,0:T(2,128)S(1)}, f32[32,2,256]{2,1,0:T(2,128)S(1)}, u32[]{:S(2)}, u32[]{:S(2)}) collective-permute-start(f32[32,2,256]{2,1,0:T(2,128)S(1)} %get-tuple-element.242), channel_id=1, source_target_pairs={{0,16},{16,32},{32,48},{48,64},{64,80},{80,96},{96,112},{1,17},{17... | collective-permute-start | bytes 196616 | tf_op jit(solution)/shard_map/ppermute | solution.py:39
  23.0 4.6 %collective-permute-start.7 = (f32[12,2]{1,0:T(8,128)S(1)}, f32[12,2]{1,0:T(8,128)S(1)}, u32[]{:S(2)}, u32[]{:S(2)}) collective-permute-start(f32[12,2]{1,0:T(8,128)S(1)} %get-tuple-element.253), channel_id=1, source_target_pairs={{1,0},{2,1},{3,2},{4,3},{5,4},{6,5},{7,6},{8,7},{9,8},{10,9},{11,1... | collective-permute-start | bytes 296 | tf_op jit(solution)/shard_map/ppermute | solution.py:42
  29.6 6.0 %collective-permute-start.3 = (f32[4,12,2]{2,1,0:T(8,128)S(1)}, f32[4,12,2]{2,1,0:T(8,128)S(1)}, u32[]{:S(2)}, u32[]{:S(2)}) collective-permute-start(f32[4,12,2]{2,1,0:T(8,128)S(1)} %get-tuple-element.245), channel_id=1, source_target_pairs={{1,0},{2,1},{3,2},{4,3},{5,4},{6,5},{7,6},{8,7},{9,8},{10,9},{11,1... | collective-permute-start | bytes 1160 | tf_op jit(solution)/shard_map/ppermute | solution.py:42
  41.1 6.3 %collective-permute-start.11 = (f32[32,12,2]{2,1,0:T(8,128)S(1)}, f32[32,12,2]{2,1,0:T(8,128)S(1)}, u32[]{:S(2)}, u32[]{:S(2)}) collective-permute-start(f32[32,12,2]{2,1,0:T(8,128)S(1)} %get-tuple-element.239), channel_id=1, source_target_pairs={{1,0},{2,1},{3,2},{4,3},{5,4},{6,5},{7,6},{8,7},{9,8},{10,9},{11,1... | collective-permute-start | bytes 9224 | tf_op jit(solution)/shard_map/ppermute | solution.py:42
  48.1 4.2 %collective-permute-done.10 = f32[32,12,2]{2,1,0:T(8,128)S(1)} collective-permute-done((f32[32,12,2]{2,1,0:T(8,128)S(1)}, f32[32,12,2]{2,1,0:T(8,128)S(1)}, u32[]{:S(2)}, u32[]{:S(2)}) %collective-permute-start.10) | collective-permute-done | bytes 3104 | tf_op jit(solution)/shard_map/ppermute | solution.py:39
  60.6 9.6 %fusion.241 = (f32[1,32,10,258]{3,2,1,0:T(8,128)}, f32[32,10,258]{2,1,0:T(8,128)S(1)}, f32[32,10,258]{2,1,0:T(8,128)S(1)}, f32[32,10,258]{2,1,0:T(8,128)S(1)}, f...) fusion(f32[2,32,12,260]{3,2,1,0:T(8,128)S(1)} %broadcast_multip, ...), kind=kLoop, calls=%fused_computation.521 | loop fusion | flops 10815360 | bytes 27130368 | tf_op jit(solution)/shard_map/stack | solution.py:77
  70.3 9.7 %fusion.242 = f32[1,32,10,258]{3,2,1,0:T(8,128)} fusion(f32[32,10,258]{2,1,0:T(8,128)} %get-tuple-element.109, f32[32,10,258]{2,1,0:T(8,128)} %get-tuple-element.108, f32[32,10,258]{2,1,0:T(8,128)} %get-tuple-element.107, f32[32,10,258]{2,1,0:T(8,128)} %get-tuple-element.106, f32[32,10,258]{2,1,0:T(8,128)} %get-tuple-element.105, ...), kind=kLoop, calls=%fused_computation.522 | loop fusion | flops 7843200 | bytes 22459392 | tf_op jit(solution)/shard_map/stack | solution.py:77
  83.3 4.4 %fusion.518 = (f32[1,32,8,256]{3,2,1,0:T(8,128)}, f32[32,8,256]{2,1,0:T(8,128)}, f32[32,8,256]{2,1,0:T(8,128)}, f32[32,8,256]{2,1,0:T(8,128)}, f32[32,8,256]{2,1...) fusion(f32[2,32,10,258]{3,2,1,0:T(8,128)S(1)} %broadcast_multip, ...), kind=kLoop, calls=%fused_computation.1103 | loop fusion | flops 8716288 | bytes 13500416 | tf_op jit(solution)/shard_map/stack | solution.py:77
  87.7 4.5 %fusion.515 = f32[1,32,8,256]{3,2,1,0:T(8,128)} fusion(f32[32,8,256]{2,1,0:T(8,128)} %get-tuple-element.84, f32[32,8,256]{2,1,0:T(8,128)} %get-tuple-element.83, f32[32,8,256]{2,1,0:T(8,128)} %get-tuple-element.82, f32[32,8,256]{2,1,0:T(8,128)} %get-tuple-element.81, f32[2,32,10,258]{3,2,1,0:T(8,128)S(1)} %broadcast_multiply_fusion.4, ...), kind=kLoop, calls=%fused_computation.1100 | loop fusion | flops 6619136 | bytes 11141120 | tf_op jit(solution)/shard_map/stack | solution.py:77
  108.6 4.7 %collective-permute-start.15 = (f32[12,2]{1,0:T(8,128)S(1)}, f32[12,2]{1,0:T(8,128)S(1)}, u32[]{:S(2)}, u32[]{:S(2)}) collective-permute-start(f32[12,2]{1,0:T(8,128)S(1)} %get-tuple-element.251), channel_id=1, source_target_pairs={{1,0},{2,1},{3,2},{4,3},{5,4},{6,5},{7,6},{8,7},{9,8},{10,9},{11,1... | collective-permute-start | bytes 296 | tf_op jit(solution)/shard_map/ppermute | solution.py:42
  118.2 8.8 %fusion.244 = f32[1,32,10,258]{3,2,1,0:T(8,128)} fusion(f32[32,10,258]{2,1,0:T(8,128)} %get-tuple-element.109, f32[32,10,258]{2,1,0:T(8,128)} %get-tuple-element.108, f32[32,10,258]{2,1,0:T(8,128)} %get-tuple-element.107, f32[32,10,258]{2,1,0:T(8,128)} %get-tuple-element.106, f32[32,10,258]{2,1,0:T(8,128)} %get-tuple-element.105, ...), kind=kLoop, calls=%fused_computation.524 | loop fusion | flops 7843200 | bytes 22003200 | tf_op jit(solution)/shard_map/stack | solution.py:77
  127.0 8.6 %fusion.243 = f32[1,32,10,258]{3,2,1,0:T(8,128)} fusion(f32[32,10,258]{2,1,0:T(8,128)} %get-tuple-element.109, f32[32,10,258]{2,1,0:T(8,128)} %get-tuple-element.108, f32[32,10,258]{2,1,0:T(8,128)} %get-tuple-element.107, f32[32,10,258]{2,1,0:T(8,128)} %get-tuple-element.106, f32[32,10,258]{2,1,0:T(8,128)} %get-tuple-element.105, ...), kind=kLoop, calls=%fused_computation.523 | loop fusion | flops 7843200 | bytes 22459392 | tf_op jit(solution)/shard_map/stack | solution.py:77
  138.1 4.5 %fusion.516 = f32[1,32,8,256]{3,2,1,0:T(8,128)} fusion(f32[32,8,256]{2,1,0:T(8,128)} %get-tuple-element.84, f32[32,8,256]{2,1,0:T(8,128)} %get-tuple-element.83, f32[32,8,256]{2,1,0:T(8,128)} %get-tuple-element.82, f32[32,8,256]{2,1,0:T(8,128)} %get-tuple-element.81, f32[2,32,10,258]{3,2,1,0:T(8,128)S(1)} %broadcast_multiply_fusion.2, ...), kind=kLoop, calls=%fused_computation.1101 | loop fusion | flops 6619136 | bytes 11141120 | tf_op jit(solution)/shard_map/stack | solution.py:77
  142.6 4.5 %fusion.519 = f32[1,32,8,256]{3,2,1,0:T(8,128)} fusion(f32[32,8,256]{2,1,0:T(8,128)} %get-tuple-element.84, f32[2,32,10,258]{3,2,1,0:T(8,128)S(1)} %broadcast_multiply_fusion.2, f32[32,8,256]{2,1,0:T(8,128)} %get-tuple-element.83, f32[32,8,256]{2,1,0:T(8,128)} %get-tuple-element.82, f32[32,8,256]{2,1,0:T(8,128)} %get-tuple-element.81, ...), kind=kLoop, calls=%fused_computation.1104 | loop fusion | flops 6619136 | bytes 11141120 | tf_op jit(solution)/shard_map/stack | solution.py:77
  158.7 12.5 %all-reduce.31 = (f32[4]{0:T(128)}, f32[4]{0:T(128)}) all-reduce(f32[4]{0:T(128)} %dynamic-update-slice.9, f32[4]{0:T(128)} %dynamic-update-slice.13), channel_id=1, replica_groups=mesh['gx_0'=4,'gx_1'=2,'gy_0'=4,'gy_1'=4] {'gx_0'}, use_global_device_ids=true, to_apply=%add.10 | all-reduce | flops 8 | bytes 64
  193.7 9.3 %all-reduce.29 = (f32[4]{0:T(128)}, f32[4]{0:T(128)}) all-reduce(f32[4]{0:T(128)} %dynamic-update-slice.11, f32[4]{0:T(128)} %dynamic-update-slice.15), channel_id=1, replica_groups=mesh['gx_0'=4,'gx_1'=2,'gy_0'=4,'gy_1'=4] {'gy_0'}, use_global_device_ids=true, to_apply=%add.12 | all-reduce | flops 8 | bytes 64
  211.4 12.6 %all-reduce.27 = (f32[4]{0:T(128)}, f32[4]{0:T(128)}) all-reduce(f32[4]{0:T(128)} %dynamic-update-slice.12, f32[4]{0:T(128)} %dynamic-update-slice.16), channel_id=1, replica_groups=mesh['gx_0'=4,'gx_1'=2,'gy_0'=4,'gy_1'=4] {'gy_1'}, use_global_device_ids=true, to_apply=%add.13 | all-reduce | flops 8 | bytes 64
  235.3 6.3 %collective-permute-start.19 = (f32[12,2]{1,0:T(8,128)S(1)}, f32[12,2]{1,0:T(8,128)S(1)}, u32[]{:S(2)}, u32[]{:S(2)}) collective-permute-start(f32[12,2]{1,0:T(8,128)S(1)} %get-tuple-element.249), channel_id=1, source_target_pairs={{1,0},{2,1},{3,2},{4,3},{5,4},{6,5},{7,6},{8,7},{9,8},{10,9},{11,1... | collective-permute-start | bytes 296 | tf_op jit(solution)/shard_map/ppermute | solution.py:42
  245.5 8.8 %fusion.246 = f32[1,32,10,258]{3,2,1,0:T(8,128)} fusion(f32[32,10,258]{2,1,0:T(8,128)} %get-tuple-element.109, f32[32,10,258]{2,1,0:T(8,128)} %get-tuple-element.108, f32[32,10,258]{2,1,0:T(8,128)} %get-tuple-element.107, f32[32,10,258]{2,1,0:T(8,128)} %get-tuple-element.106, f32[32,10,258]{2,1,0:T(8,128)} %get-tuple-element.105, ...), kind=kLoop, calls=%fused_computation.526 | loop fusion | flops 7843200 | bytes 22003200 | tf_op jit(solution)/shard_map/stack | solution.py:77
  254.3 8.6 %fusion.245 = f32[1,32,10,258]{3,2,1,0:T(8,128)} fusion(f32[32,10,258]{2,1,0:T(8,128)} %get-tuple-element.109, f32[32,10,258]{2,1,0:T(8,128)} %get-tuple-element.108, f32[32,10,258]{2,1,0:T(8,128)} %get-tuple-element.107, f32[32,10,258]{2,1,0:T(8,128)} %get-tuple-element.106, f32[32,10,258]{2,1,0:T(8,128)} %get-tuple-element.105, ...), kind=kLoop, calls=%fused_computation.525 | loop fusion | flops 7843200 | bytes 22459392 | tf_op jit(solution)/shard_map/stack | solution.py:77
  280.8 10.0 %all-reduce.30 = (f32[4]{0:T(128)S(1)}, f32[4]{0:T(128)S(1)}) all-reduce(f32[4]{0:T(128)S(1)} %dynamic-update-slice.17, f32[4]{0:T(128)S(1)} %dynamic-update-slice.21), channel_id=1, replica_groups=mesh['gx_0'=4,'gx_1'=2,'gy_0'=4,'gy_1'=4] {'gx_0'}, use_global_device_ids=true, to_apply=%add.18 | all-reduce | flops 8 | bytes 64
  301.1 7.2 %all-reduce.28 = (f32[4]{0:T(128)S(1)}, f32[4]{0:T(128)S(1)}) all-reduce(f32[4]{0:T(128)S(1)} %dynamic-update-slice.19, f32[4]{0:T(128)S(1)} %dynamic-update-slice.23), channel_id=1, replica_groups=mesh['gx_0'=4,'gx_1'=2,'gy_0'=4,'gy_1'=4] {'gy_0'}, use_global_device_ids=true, to_apply=%add.20 | all-reduce | flops 8 | bytes 64
  312.2 13.1 %all-reduce.26 = (f32[4]{0:T(128)S(1)}, f32[4]{0:T(128)S(1)}) all-reduce(f32[4]{0:T(128)S(1)} %dynamic-update-slice.20, f32[4]{0:T(128)S(1)} %dynamic-update-slice.24), channel_id=1, replica_groups=mesh['gx_0'=4,'gx_1'=2,'gy_0'=4,'gy_1'=4] {'gy_1'}, use_global_device_ids=true, to_apply=%add.21 | all-reduce | flops 8 | bytes 64
  (328 shorter events, 146.2 us)
Async XLA Ops:
  1.4 16.1 %collective-permute-start.4 = (f32[2,256]{1,0:T(2,128)S(1)}, f32[2,256]{1,0:T(2,128)S(1)}, u32[]{:S(2)}, u32[]{:S(2)}) collective-permute-start(f32[2,256]{1,0:T(2,128)S(1)} %get-tuple-element.261), channel_id=1, source_target_pairs={{0,16},{16,32},{32,48},{48,64},{64,80},{80,96},{96,112},{1,17},{17... | collective-permute-start | bytes 6152 | tf_op jit(solution)/shard_map/ppermute | solution.py:39
  3.1 15.7 %collective-permute-start.5 = (f32[2,256]{1,0:T(2,128)S(1)}, f32[2,256]{1,0:T(2,128)S(1)}, u32[]{:S(2)}, u32[]{:S(2)}) collective-permute-start(f32[2,256]{1,0:T(2,128)S(1)} %get-tuple-element.262), channel_id=1, source_target_pairs={{16,0},{32,16},{48,32},{64,48},{80,64},{96,80},{112,96},{17,1},{33... | collective-permute-start | bytes 6152 | tf_op jit(solution)/shard_map/ppermute | solution.py:42
  5.2 88.2 %copy-start.52 = (f32[8,256]{1,0:T(8,128)}, f32[8,256]{1,0:T(8,128)S(1)}, u32[]{:S(2)}) copy-start(f32[8,256]{1,0:T(8,128)S(1)} %get-tuple-element.255) | copy-start | bytes 24580
  5.9 47.6 %copy-start.12 = (f32[32,8,256]{2,1,0:T(8,128)S(1)}, f32[32,8,256]{2,1,0:T(8,128)}, u32[]{:S(2)}) copy-start(f32[32,8,256]{2,1,0:T(8,128)} %param.16) | copy-start | bytes 786436
  5.9 17.1 %collective-permute-start = (f32[4,2,256]{2,1,0:T(2,128)S(1)}, f32[4,2,256]{2,1,0:T(2,128)S(1)}, u32[]{:S(2)}, u32[]{:S(2)}) collective-permute-start(f32[4,2,256]{2,1,0:T(2,128)S(1)} %get-tuple-element.246), channel_id=1, source_target_pairs={{0,16},{16,32},{32,48},{48,64},{64,80},{80,96},{96,112},{1,17},{17... | collective-permute-start | bytes 24584 | tf_op jit(solution)/shard_map/ppermute | solution.py:39
  10.8 16.8 %collective-permute-start.1 = (f32[4,2,256]{2,1,0:T(2,128)S(1)}, f32[4,2,256]{2,1,0:T(2,128)S(1)}, u32[]{:S(2)}, u32[]{:S(2)}) collective-permute-start(f32[4,2,256]{2,1,0:T(2,128)S(1)} %get-tuple-element.247), channel_id=1, source_target_pairs={{16,0},{32,16},{48,32},{64,48},{80,64},{96,80},{112,96},{17,1},{33... | collective-permute-start | bytes 24584 | tf_op jit(solution)/shard_map/ppermute | solution.py:42
  13.2 24.2 %collective-permute-start.8 = (f32[32,2,256]{2,1,0:T(2,128)S(1)}, f32[32,2,256]{2,1,0:T(2,128)S(1)}, u32[]{:S(2)}, u32[]{:S(2)}) collective-permute-start(f32[32,2,256]{2,1,0:T(2,128)S(1)} %get-tuple-element.242), channel_id=1, source_target_pairs={{0,16},{16,32},{32,48},{48,64},{64,80},{80,96},{96,112},{1,17},{17... | collective-permute-start | bytes 196616 | tf_op jit(solution)/shard_map/ppermute | solution.py:39
  17.5 36.6 %copy-start.61 = (f32[2,256]{1,0:T(2,128)}, f32[2,256]{1,0:T(2,128)S(1)}, u32[]{:S(2)}) copy-start(f32[2,256]{1,0:T(2,128)S(1)} %collective-permute-done.4) | copy-start | bytes 6148
  17.5 20.5 %collective-permute-start.9 = (f32[32,2,256]{2,1,0:T(2,128)S(1)}, f32[32,2,256]{2,1,0:T(2,128)S(1)}, u32[]{:S(2)}, u32[]{:S(2)}) collective-permute-start(f32[32,2,256]{2,1,0:T(2,128)S(1)} %get-tuple-element.243), channel_id=1, source_target_pairs={{16,0},{32,16},{48,32},{64,48},{80,64},{96,80},{112,96},{17,1},{33... | collective-permute-start | bytes 196616 | tf_op jit(solution)/shard_map/ppermute | solution.py:42
  18.8 35.3 %copy-start.63 = (f32[2,256]{1,0:T(2,128)}, f32[2,256]{1,0:T(2,128)S(1)}, u32[]{:S(2)}) copy-start(f32[2,256]{1,0:T(2,128)S(1)} %collective-permute-done.5) | copy-start | bytes 6148
  19.6 10.0 %collective-permute-start.6 = (f32[12,2]{1,0:T(8,128)S(1)}, f32[12,2]{1,0:T(8,128)S(1)}, u32[]{:S(2)}, u32[]{:S(2)}) collective-permute-start(f32[12,2]{1,0:T(8,128)S(1)} %get-tuple-element.252), channel_id=1, source_target_pairs={{0,1},{1,2},{2,3},{3,4},{4,5},{5,6},{6,7},{7,8},{8,9},{9,10},{10,1... | collective-permute-start | bytes 296 | tf_op jit(solution)/shard_map/ppermute | solution.py:39
  23.0 12.7 %collective-permute-start.7 = (f32[12,2]{1,0:T(8,128)S(1)}, f32[12,2]{1,0:T(8,128)S(1)}, u32[]{:S(2)}, u32[]{:S(2)}) collective-permute-start(f32[12,2]{1,0:T(8,128)S(1)} %get-tuple-element.253), channel_id=1, source_target_pairs={{1,0},{2,1},{3,2},{4,3},{5,4},{6,5},{7,6},{8,7},{9,8},{10,9},{11,1... | collective-permute-start | bytes 296 | tf_op jit(solution)/shard_map/ppermute | solution.py:42
  27.7 8.8 %collective-permute-start.2 = (f32[4,12,2]{2,1,0:T(8,128)S(1)}, f32[4,12,2]{2,1,0:T(8,128)S(1)}, u32[]{:S(2)}, u32[]{:S(2)}) collective-permute-start(f32[4,12,2]{2,1,0:T(8,128)S(1)} %get-tuple-element.244), channel_id=1, source_target_pairs={{0,1},{1,2},{2,3},{3,4},{4,5},{5,6},{6,7},{7,8},{8,9},{9,10},{10,1... | collective-permute-start | bytes 1160 | tf_op jit(solution)/shard_map/ppermute | solution.py:39
  29.6 7.6 %collective-permute-start.3 = (f32[4,12,2]{2,1,0:T(8,128)S(1)}, f32[4,12,2]{2,1,0:T(8,128)S(1)}, u32[]{:S(2)}, u32[]{:S(2)}) collective-permute-start(f32[4,12,2]{2,1,0:T(8,128)S(1)} %get-tuple-element.245), channel_id=1, source_target_pairs={{1,0},{2,1},{3,2},{4,3},{5,4},{6,5},{7,6},{8,7},{9,8},{10,9},{11,1... | collective-permute-start | bytes 1160 | tf_op jit(solution)/shard_map/ppermute | solution.py:42
  39.2 13.2 %collective-permute-start.10 = (f32[32,12,2]{2,1,0:T(8,128)S(1)}, f32[32,12,2]{2,1,0:T(8,128)S(1)}, u32[]{:S(2)}, u32[]{:S(2)}) collective-permute-start(f32[32,12,2]{2,1,0:T(8,128)S(1)} %get-tuple-element.238), channel_id=1, source_target_pairs={{0,1},{1,2},{2,3},{3,4},{4,5},{5,6},{6,7},{7,8},{8,9},{9,10},{10,1... | collective-permute-start | bytes 9224 | tf_op jit(solution)/shard_map/ppermute | solution.py:39
  41.1 12.4 %collective-permute-start.11 = (f32[32,12,2]{2,1,0:T(8,128)S(1)}, f32[32,12,2]{2,1,0:T(8,128)S(1)}, u32[]{:S(2)}, u32[]{:S(2)}) collective-permute-start(f32[32,12,2]{2,1,0:T(8,128)S(1)} %get-tuple-element.239), channel_id=1, source_target_pairs={{1,0},{2,1},{3,2},{4,3},{5,4},{6,5},{7,6},{8,7},{9,8},{10,9},{11,1... | collective-permute-start | bytes 9224 | tf_op jit(solution)/shard_map/ppermute | solution.py:42
  97.1 4.8 %collective-permute-start.12 = (f32[2,256]{1,0:T(2,128)}, f32[2,256]{1,0:T(2,128)}, u32[]{:S(2)}, u32[]{:S(2)}) collective-permute-start(f32[2,256]{1,0:T(2,128)} %get-tuple-element.259), channel_id=1, source_target_pairs={{0,16},{16,32},{32,48},{48,64},{64,80},{80,96},{96,112},{1,17},{17... | collective-permute-start | bytes 6152 | tf_op jit(solution)/shard_map/ppermute | solution.py:39
  99.1 4.8 %collective-permute-start.13 = (f32[2,256]{1,0:T(2,128)}, f32[2,256]{1,0:T(2,128)}, u32[]{:S(2)}, u32[]{:S(2)}) collective-permute-start(f32[2,256]{1,0:T(2,128)} %get-tuple-element.260), channel_id=1, source_target_pairs={{16,0},{32,16},{48,32},{64,48},{80,64},{96,80},{112,96},{17,1},{33... | collective-permute-start | bytes 6152 | tf_op jit(solution)/shard_map/ppermute | solution.py:42
  104.7 8.6 %collective-permute-start.14 = (f32[12,2]{1,0:T(8,128)S(1)}, f32[12,2]{1,0:T(8,128)S(1)}, u32[]{:S(2)}, u32[]{:S(2)}) collective-permute-start(f32[12,2]{1,0:T(8,128)S(1)} %get-tuple-element.250), channel_id=1, source_target_pairs={{0,1},{1,2},{2,3},{3,4},{4,5},{5,6},{6,7},{7,8},{8,9},{9,10},{10,1... | collective-permute-start | bytes 296 | tf_op jit(solution)/shard_map/ppermute | solution.py:39
  108.6 6.1 %collective-permute-start.15 = (f32[12,2]{1,0:T(8,128)S(1)}, f32[12,2]{1,0:T(8,128)S(1)}, u32[]{:S(2)}, u32[]{:S(2)}) collective-permute-start(f32[12,2]{1,0:T(8,128)S(1)} %get-tuple-element.251), channel_id=1, source_target_pairs={{1,0},{2,1},{3,2},{4,3},{5,4},{6,5},{7,6},{8,7},{9,8},{10,9},{11,1... | collective-permute-start | bytes 296 | tf_op jit(solution)/shard_map/ppermute | solution.py:42
  228.9 2.6 collective-permute-start.16
  230.2 3.1 collective-permute-start.17
  233.3 8.2 %collective-permute-start.18 = (f32[12,2]{1,0:T(8,128)S(1)}, f32[12,2]{1,0:T(8,128)S(1)}, u32[]{:S(2)}, u32[]{:S(2)}) collective-permute-start(f32[12,2]{1,0:T(8,128)S(1)} %get-tuple-element.248), channel_id=1, source_target_pairs={{0,1},{1,2},{2,3},{3,4},{4,5},{5,6},{6,7},{7,8},{8,9},{9,10},{10,1... | collective-permute-start | bytes 296 | tf_op jit(solution)/shard_map/ppermute | solution.py:39
  235.3 7.4 %collective-permute-start.19 = (f32[12,2]{1,0:T(8,128)S(1)}, f32[12,2]{1,0:T(8,128)S(1)}, u32[]{:S(2)}, u32[]{:S(2)}) collective-permute-start(f32[12,2]{1,0:T(8,128)S(1)} %get-tuple-element.249), channel_id=1, source_target_pairs={{1,0},{2,1},{3,2},{4,3},{5,4},{6,5},{7,6},{8,7},{9,8},{10,9},{11,1... | collective-permute-start | bytes 296 | tf_op jit(solution)/shard_map/ppermute | solution.py:42
  (62 other events, 392.6 us)
